TPU v7x, 32 devices: a whole 2x2x4 slice. The times are simulated.
32 devices in a mesh: rows: 8 (over y, x, core), cols: 4 (over z).
Axes of the slice: x: 2, y: 2, z: 4, core: 2. Of those that a mesh axis runs over, the one named last changes fastest.
Arguments:
- coarse: float32 [512, 512], P('rows', 'cols'), may hold values from -6 to 6
- detail4: float32 [3, 512, 512], P(None, 'rows', 'cols'), may hold values from -6 to 6
- detail3: float32 [3, 1024, 1024], P(None, 'rows', 'cols'), may hold values from -6 to 6
- detail2: float32 [3, 2048, 2048], P(None, 'rows', 'cols'), may hold values from -6 to 6
- detail1: float32 [3, 4096, 4096], P(None, 'rows', 'cols'), may hold values from -6 to 6
Outputs:
- image: float32 [8192, 8192], P('rows', 'cols')
All inputs are finite; a program needn't handle non-finite values.
Results may differ from a plain program's by a relative error of at most 0.00013.
Values sent between devices are 32-bit elements; how exact they have to be, the bound alone decides.
A program may use at most 128 MiB of HBM per device.

v0:
```python
import functools

import jax
import jax.numpy as jnp
from jax import lax
from jax.experimental import pallas as pl
from jax.experimental.pallas import tpu as pltpu
from jax.sharding import PartitionSpec as P

lift_alpha = -1.586134342059924
lift_beta = -0.052980118572961
lift_gamma = 0.882911075530934
lift_delta = 0.443506852043971
lift_scale = 1.149604398860241

MESH = pl.DeviceIdType.MESH
LANES = 128
SUB = 8


def groups_of(height):
    return min(16, height // SUB)


def lanes_of(shape):
    return lax.broadcasted_iota(jnp.int32, shape, len(shape) - 1)


def rows_of(shape):
    return lax.broadcasted_iota(jnp.int32, shape, len(shape) - 2)


def exchange(mesh_shape, levels, *refs):
    count = len(levels)
    inputs, refs = refs[:count], refs[count:]
    below, above, refs = refs[:count], refs[count : 2 * count], refs[2 * count :]
    from_right, from_left, down_right, down_left, up_right, up_left, *refs = refs
    packed, top, bottom, *refs = refs
    firsts, lasts, refs = refs[:count], refs[count : 2 * count], refs[2 * count :]
    local_sem, send_sem, recv_sem = refs

    n_rows, n_cols = mesh_shape
    row, col = lax.axis_index("rows"), lax.axis_index("cols")
    row_next, row_prev = lax.rem(row + 1, n_rows), lax.rem(row + n_rows - 1, n_rows)
    col_next, col_prev = lax.rem(col + 1, n_cols), lax.rem(col + n_cols - 1, n_cols)

    barrier = pltpu.get_barrier_semaphore()
    neighbours = [
        (r, c)
        for r in (row_prev, row, row_next)
        for c in (col_prev, col, col_next)
        if not (r is row and c is col)
    ]
    for place in neighbours:
        pl.semaphore_signal(barrier, inc=1, device_id=place, device_id_type=MESH)

    loads = []
    for i, (bands, height, width) in enumerate(levels):
        for j, (slab, start) in enumerate(((firsts[i], 0), (lasts[i], width - LANES))):
            copy = pltpu.make_async_copy(
                inputs[i].at[:, :, pl.ds(start, LANES)], slab, local_sem.at[2 * i + j]
            )
            copy.start()
            loads.append(copy)

    pl.semaphore_wait(barrier, len(neighbours))

    sends = []

    def send(src, dst, place):
        k = len(sends)
        copy = pltpu.make_async_remote_copy(
            src_ref=src,
            dst_ref=dst,
            send_sem=send_sem.at[k],
            recv_sem=recv_sem.at[k],
            device_id=place,
            device_id_type=MESH,
        )
        copy.start()
        sends.append(copy)

    for i in reversed(range(count)):
        height = levels[i][1]
        send(inputs[i].at[:, pl.ds(0, SUB), :], below[i], (row_prev, col))
        send(inputs[i].at[:, pl.ds(height - SUB, SUB), :], above[i], (row_next, col))

    for copy in loads:
        copy.wait()

    tops = bottoms = None
    offset = place = 0
    for i, (bands, height, width) in enumerate(levels):
        groups = groups_of(height)
        part = height // groups
        lane = lanes_of((part, LANES))
        slot = lax.rem(lane + 4, LANES) // 8
        lane8 = lanes_of((SUB, LANES))
        slot8 = lax.rem(lane8 + 4, LANES) // 8
        for b in range(bands):
            total = None
            for g in range(groups):
                rows = pl.ds(g * part, part)
                edge = jnp.where(lane < 64, firsts[i][b, rows, :], lasts[i][b, rows, :])
                if g:
                    edge = pltpu.roll(edge, 8 * g, 1)
                total = edge if total is None else jnp.where(slot == g, edge, total)
            packed[pl.ds(offset, part), :] = total
            offset += part
            for end in range(2):
                rows = pl.ds(0 if end == 0 else height - SUB, SUB)
                edge = jnp.where(lane8 < 64, firsts[i][b, rows, :], lasts[i][b, rows, :])
                if place:
                    edge = pltpu.roll(edge, 8 * place, 1)
                if end == 0:
                    tops = edge if tops is None else jnp.where(slot8 == place, edge, tops)
                else:
                    bottoms = edge if bottoms is None else jnp.where(slot8 == place, edge, bottoms)
            place += 1
    top[...] = tops
    bottom[...] = bottoms

    send(packed, from_right, (row, col_prev))
    send(packed, from_left, (row, col_next))
    send(top, down_right, (row_prev, col_prev))
    send(top, down_left, (row_prev, col_next))
    send(bottom, up_right, (row_next, col_prev))
    send(bottom, up_left, (row_next, col_next))
    for copy in sends:
        copy.wait()


def lifted(smooth, rough, before, after):
    smooth = smooth - lift_delta * (rough + before(rough))
    rough = rough - lift_gamma * (smooth + after(smooth))
    smooth = smooth - lift_beta * (rough + before(rough))
    rough = rough - lift_alpha * (smooth + after(smooth))
    return smooth, rough


def synthesis(sizes, chunk_rows, *refs):
    count = len(sizes)
    arrays = count + 1
    inputs, refs = refs[:arrays], refs[arrays:]
    below, above, refs = refs[:arrays], refs[arrays : 2 * arrays], refs[2 * arrays :]
    from_right, from_left, down_right, down_left, up_right, up_left, out, *refs = refs
    bands, joined, refs = refs[:count], refs[count], refs[count + 1 :]
    finished, load_sem, store_sem = refs

    loads = []
    k = 0
    for level, (height, width) in enumerate(sizes):
        mine = []
        for c in range(width // LANES):
            columns = pl.ds(c * LANES, LANES)
            if level == 0:
                copy = pltpu.make_async_copy(
                    inputs[0].at[:, :, columns],
                    bands[0].at[pl.ds(0, 1), c, pl.ds(0, height), :],
                    load_sem.at[k],
                )
                copy.start()
                mine.append(copy)
                k += 1
            copy = pltpu.make_async_copy(
                inputs[level + 1].at[:, :, columns],
                bands[level].at[pl.ds(1, 3), c, pl.ds(0, height), :],
                load_sem.at[k],
            )
            copy.start()
            mine.append(copy)
            k += 1
        loads.append(mine)

    lane = lanes_of((SUB, LANES))
    sub = rows_of((SUB, LANES))
    even = lax.rem(lane, 2) == 0
    low = lane < 64
    pick_low = lane // 2 + jnp.where(even, 0, 64)
    pick_high = lane // 2 + jnp.where(even, 64, 0)
    right_side = lax.rem(lane, 8) < 4

    corner = jnp.where(
        sub < 4,
        jnp.where(right_side, down_right[...], down_left[...]),
        jnp.where(right_side, up_right[...], up_left[...]),
    )
    offset = place = 0
    for i in range(arrays):
        level = max(i - 1, 0)
        height, width = sizes[level]
        groups = groups_of(height)
        part = height // groups
        tiles = width // LANES
        wide = lax.rem(lanes_of((part, LANES)), 8) < 4
        for b in range(1 if i == 0 else 3):
            ref = bands[level].at[b if i == 0 else b + 1]
            rows = pl.ds(offset, part)
            edge = jnp.where(wide, from_right[rows, :], from_left[rows, :])
            for g in range(groups):
                ref[tiles, pl.ds(g * part, part), :] = (
                    pltpu.roll(edge, LANES - 8 * g, 1) if g else edge
                )
            offset += part
            for c in range(tiles):
                columns = pl.ds(c * LANES, LANES)
                ref[c, pl.ds(height, SUB), :] = jnp.where(
                    sub < 4, below[i][b, :, columns], above[i][b, :, columns]
                )
            ref[tiles, pl.ds(height, SUB), :] = (
                pltpu.roll(corner, LANES - 8 * place, 1) if place else corner
            )
            place += 1

    big, small = lift_scale * lift_scale, 1.0 / (lift_scale * lift_scale)

    def vertical(ref, c, start, length, before, after):
        def window(b):
            body = ref[b, c, pl.ds(start, length), :]
            halo = jnp.where(
                sub < 4, ref[b, c, pl.ds(after, SUB), :], ref[b, c, pl.ds(before, SUB), :]
            )
            return jnp.concatenate([body, halo], axis=0)

        total = length + SUB
        shift_down = lambda x: pltpu.roll(x, 1, 0)
        shift_up = lambda x: pltpu.roll(x, total - 1, 0)
        for half, (s, r) in enumerate(((0, 2), (1, 3))):
            smooth, rough = window(s), window(r)
            if half == 0:
                smooth = smooth * big
            else:
                rough = rough * small
            smooth, rough = lifted(smooth, rough, shift_down, shift_up)
            joined[half, c, pl.ds(0, length, stride=2), :] = smooth[:length]
            joined[half, c, pl.ds(1, length, stride=2), :] = rough[:length]

    def horizontal(tiles, load, store, last):
        smooth = [load(0, c) for c in range(tiles + 1)]
        rough = [load(1, c) for c in range(tiles + 1)]

        def before(x):
            turned = [pltpu.roll(t, 1, 1) for t in x]
            return [jnp.where(lane == 0, turned[c - 1], turned[c]) for c in range(tiles + 1)]

        def after(x):
            turned = [pltpu.roll(t, LANES - 1, 1) for t in x]
            return [
                jnp.where(lane == LANES - 1, turned[(c + 1) % (tiles + 1)], turned[c])
                for c in range(tiles + 1)
            ]

        def step(x, factor, y, z):
            return [a - factor * (b + c) for a, b, c in zip(x, y, z)]

        smooth = step(smooth, lift_delta, rough, before(rough))
        rough = step(rough, lift_gamma, smooth, after(smooth))
        smooth = step(smooth, lift_beta, rough, before(rough))
        rough = step(rough, lift_alpha, smooth, after(smooth))
        for c in range(tiles if last else tiles + 1):
            first = jnp.where(low, smooth[c], rough[c])
            second = jnp.where(low, rough[c], smooth[c])
            first = jnp.take_along_axis(first, pick_low, axis=1, mode="promise_in_bounds")
            second = jnp.take_along_axis(second, pick_high, axis=1, mode="promise_in_bounds")
            left = jnp.where(even, first, second)
            right = jnp.where(even, second, first)
            if c < tiles:
                store(2 * c, left)
                store(2 * c + 1, right)
            else:
                store(2 * c, jnp.where(low, left, right))

    stores = []
    for level, (height, width) in enumerate(sizes):
        tiles = width // LANES
        last = level == count - 1
        rows = min(chunk_rows, height)
        chunks = height // rows
        ref = bands[level]
        target = finished if last else bands[level + 1].at[0]
        for copy in loads[level]:
            copy.wait()

        def one_chunk(i, carry):
            start = pl.multiple_of(i * rows, SUB)
            before = pl.multiple_of(jnp.where(i == 0, height, start - SUB), SUB)
            after = pl.multiple_of(start + rows, SUB)

            def one_column(c, carry):
                vertical(ref, c, start, rows, before, after)
                return carry

            lax.fori_loop(0, tiles + 1, one_column, 0)

            def one_row(t, carry):
                where = pl.ds(pl.multiple_of(t * SUB, SUB), SUB)
                into = pl.ds(pl.multiple_of(2 * start + t * SUB, SUB), SUB)

                def store(c, value):
                    target[c, into, :] = value

                horizontal(tiles, lambda half, c: joined[half, c, where, :], store, last)
                return carry

            lax.fori_loop(0, 2 * rows // SUB, one_row, 0)
            return carry

        if last:
            for i in range(chunks):
                one_chunk(i, 0)
                span = pl.ds(2 * i * rows, 2 * rows)
                for c in range(2 * tiles):
                    copy = pltpu.make_async_copy(
                        finished.at[c, span, :],
                        out.at[span, pl.ds(c * LANES, LANES)],
                        store_sem.at[len(stores)],
                    )
                    copy.start()
                    stores.append(copy)
        else:
            lax.fori_loop(0, chunks, one_chunk, 0)

            def edge_column(c, carry):
                vertical(ref, c, height, SUB, height - SUB, 0)
                return carry

            lax.fori_loop(0, tiles + 1, edge_column, 0)

            def load(half, c):
                return jnp.where(
                    sub < 4, joined[half, c, pl.ds(0, SUB), :], joined[half, c, pl.ds(SUB, SUB), :]
                )

            def store(c, value):
                target[c, pl.ds(2 * height, SUB), :] = value

            horizontal(tiles, load, store, False)
    for copy in stores:
        copy.wait()


def per_device(mesh_shape, coarse, *details):
    arrays = (coarse[None],) + details
    levels = [a.shape for a in arrays]
    sizes = [d.shape[1:] for d in details]
    f32 = jnp.float32
    shape = lambda *dims: jax.ShapeDtypeStruct(dims, f32)
    packed_rows = sum(b * (h // groups_of(h)) for b, h, w in levels)
    strips = [shape(b, SUB, w) for b, h, w in levels]
    anywhere = pl.BlockSpec(memory_space=pl.ANY)
    in_vmem = pl.BlockSpec(memory_space=pltpu.VMEM)
    n = len(levels)
    halo_shapes = strips + strips + [shape(packed_rows, LANES)] * 2 + [shape(SUB, LANES)] * 4
    n_sends = 2 * n + 6
    halos = pl.pallas_call(
        functools.partial(exchange, mesh_shape, levels),
        out_shape=halo_shapes,
        in_specs=[anywhere] * n,
        out_specs=[anywhere] * len(halo_shapes),
        scratch_shapes=[
            pltpu.VMEM((packed_rows, LANES), f32),
            pltpu.VMEM((SUB, LANES), f32),
            pltpu.VMEM((SUB, LANES), f32),
        ]
        + [pltpu.VMEM((b, h, LANES), f32) for b, h, w in levels] * 2
        + [
            pltpu.SemaphoreType.DMA((2 * n,)),
            pltpu.SemaphoreType.DMA((n_sends,)),
            pltpu.SemaphoreType.DMA((n_sends,)),
        ],
        compiler_params=pltpu.CompilerParams(collective_id=0, has_side_effects=True),
        name="exchange",
    )(*arrays)

    chunk_rows = 64
    height, width = sizes[-1]
    n_loads = sum(w // LANES for h, w in sizes) + sizes[0][1] // LANES
    n_stores = (height // min(chunk_rows, height)) * (2 * width // LANES)
    return pl.pallas_call(
        functools.partial(synthesis, sizes, chunk_rows),
        out_shape=shape(2 * height, 2 * width),
        in_specs=[anywhere] * n + [in_vmem] * len(halo_shapes),
        out_specs=anywhere,
        scratch_shapes=[
            pltpu.VMEM((4, w // LANES + 1, h + SUB, LANES), f32) for h, w in sizes
        ]
        + [
            pltpu.VMEM((2, width // LANES + 1, 2 * min(chunk_rows, height), LANES), f32),
            pltpu.VMEM((2 * width // LANES, 2 * height, LANES), f32),
            pltpu.SemaphoreType.DMA((n_loads,)),
            pltpu.SemaphoreType.DMA((n_stores,)),
        ],
        compiler_params=pltpu.CompilerParams(vmem_limit_bytes=56 * 1024 * 1024),
        name="synthesis",
    )(*arrays, *halos)


def solution(mesh):
    mesh_shape = (mesh.shape["rows"], mesh.shape["cols"])
    return jax.shard_map(
        functools.partial(per_device, mesh_shape),
        mesh=mesh,
        in_specs=(
            P("rows", "cols"),
            P(None, "rows", "cols"),
            P(None, "rows", "cols"),
            P(None, "rows", "cols"),
            P(None, "rows", "cols"),
        ),
        out_specs=P("rows", "cols"),
        check_vma=False,
    )
```

profile of v0, /device:TPU:0, one launch (start us, length us, event | category | flops | bytes accessed | tf_op | source)
XLA Modules:
  0.0 119.3 jit_solution(14045297813397287771)
XLA Ops:
  0.0 14.4 %exchange.1 = (f32[1,8,128]{2,1,0:T(8,128)}, f32[3,8,128]{2,1,0:T(8,128)}, f32[3,8,256]{2,1,0:T(8,128)}, f32[3,8,512]{2,1,0:T(8,128)}, f32[3,8,1024]{2,1,0:T(8,1...) custom-call(f32[1,64,128]{2,1,0:T(8,128)} %bitcast.1, ...), custom_call_target="tpu_custom_call" | custom-call | tf_op jit(solution)/shard_map/exchange/pallas_call | solution.py:355
  14.4 104.9 %synthesis.1 = f32[1024,2048]{1,0:T(8,128)} custom-call(f32[1,64,128]{2,1,0:T(8,128)} %bitcast.2, f32[3,64,128]{2,1,0:T(8,128)} %refs_1_.3, f32[3,128,256]{2,1,0:T(8,128)} %refs_2_.3, f32[3,256,512]{2,1,0:T(8,128)} %refs_3_.3, f32[3,512,1024]{2,1,0:T(8,128)} %refs_4_.3, f32[1,8,128]{2,1,0:T(8,128)} %get-tuple-element.21.refs_5_, ...), custom_call_target="tpu_custom_call" | custom-call | tf_op jit(solution)/shard_map/synthesis/pallas_call | solution.py:379
where the time goes:
time: 119 us
  Pallas kernels  119 us (100%)
    pallas_call x1, Pallas kernels, per_device(): pl.pallas_call(functools.partial(synthesis, sizes, chunk_rows), out_shape...  105 us
    pallas_call x1, Pallas kernels, per_device(): pl.pallas_call(functools.partial(exchange, mesh_shape, levels), out_shape...  14.4 us

commit v1 on v0

--- a/solution.py
+++ b/solution.py
@@ -1,4 +1,5 @@
 import functools
+import math
 
 import jax
 import jax.numpy as jnp
@@ -16,6 +17,7 @@
 MESH = pl.DeviceIdType.MESH
 LANES = 128
 SUB = 8
+UNROLL = 4
 
 
 def groups_of(height):
@@ -276,6 +278,7 @@
         last = level == count - 1
         rows = min(chunk_rows, height)
         chunks = height // rows
+        unroll = math.gcd(max(UNROLL, 16 // tiles), 2 * rows // SUB)
         ref = bands[level]
         target = finished if last else bands[level + 1].at[0]
         for copy in loads[level]:
@@ -293,16 +296,21 @@
             lax.fori_loop(0, tiles + 1, one_column, 0)
 
             def one_row(t, carry):
-                where = pl.ds(pl.multiple_of(t * SUB, SUB), SUB)
-                into = pl.ds(pl.multiple_of(2 * start + t * SUB, SUB), SUB)
-
-                def store(c, value):
-                    target[c, into, :] = value
-
-                horizontal(tiles, lambda half, c: joined[half, c, where, :], store, last)
+                for u in range(unroll):
+                    first = (t * unroll + u) * SUB
+                    where = pl.ds(pl.multiple_of(first, SUB), SUB)
+                    into = pl.ds(pl.multiple_of(2 * start + first, SUB), SUB)
+
+                    def store(c, value, into=into):
+                        target[c, into, :] = value
+
+                    def load(half, c, where=where):
+                        return joined[half, c, where, :]
+
+                    horizontal(tiles, load, store, last)
                 return carry
 
-            lax.fori_loop(0, 2 * rows // SUB, one_row, 0)
+            lax.fori_loop(0, 2 * rows // (SUB * unroll), one_row, 0)
             return carry
 
         if last:

time: 119 us -> 51.7 us (0.43)
  Pallas kernels: 119 us -> 51.5 us
    pallas_call x1, Pallas kernels: 105 us -> 37.1 us  [per_device(): pl.pallas_call(functools.partial(synthesis, sizes, chunk_rows), out_shape...]
where the time goes in v1:
time: 51.7 us; the launch traced here: 51.5 us
  Pallas kernels  51.5 us (100%)
    pallas_call x1, Pallas kernels, per_device(): pl.pallas_call(functools.partial(synthesis, sizes, chunk_rows), out_shape...  37.1 us
    pallas_call x1, Pallas kernels, per_device(): pl.pallas_call(functools.partial(exchange, mesh_shape, levels), out_shape...  14.4 us

profile of v1, /device:TPU:0, one launch (start us, length us, event | category | flops | bytes accessed | tf_op | source)
XLA Modules:
  0.0 51.5 jit_solution(9229054432144474084)
XLA Ops:
  0.0 14.4 %exchange.1 = (f32[1,8,128]{2,1,0:T(8,128)}, f32[3,8,128]{2,1,0:T(8,128)}, f32[3,8,256]{2,1,0:T(8,128)}, f32[3,8,512]{2,1,0:T(8,128)}, f32[3,8,1024]{2,1,0:T(8,1...) custom-call(f32[1,64,128]{2,1,0:T(8,128)} %bitcast.1, ...), custom_call_target="tpu_custom_call" | custom-call | tf_op jit(solution)/shard_map/exchange/pallas_call | solution.py:363
  14.4 37.1 %synthesis.1 = f32[1024,2048]{1,0:T(8,128)} custom-call(f32[1,64,128]{2,1,0:T(8,128)} %bitcast.2, f32[3,64,128]{2,1,0:T(8,128)} %refs_1_.3, f32[3,128,256]{2,1,0:T(8,128)} %refs_2_.3, f32[3,256,512]{2,1,0:T(8,128)} %refs_3_.3, f32[3,512,1024]{2,1,0:T(8,128)} %refs_4_.3, f32[1,8,128]{2,1,0:T(8,128)} %get-tuple-element.21.refs_5_, ...), custom_call_target="tpu_custom_call" | custom-call | tf_op jit(solution)/shard_map/synthesis/pallas_call | solution.py:387

commit v2 on v1

--- a/solution.py
+++ b/solution.py
@@ -140,14 +140,14 @@
     return smooth, rough
 
 
-def synthesis(sizes, chunk_rows, *refs):
+def synthesis(sizes, chunk_rows, piece_rows, *refs):
     count = len(sizes)
     arrays = count + 1
     inputs, refs = refs[:arrays], refs[arrays:]
     below, above, refs = refs[:arrays], refs[arrays : 2 * arrays], refs[2 * arrays :]
     from_right, from_left, down_right, down_left, up_right, up_left, out, *refs = refs
     bands, joined, refs = refs[:count], refs[count], refs[count + 1 :]
-    finished, load_sem, store_sem = refs
+    finished, load_sem, store_sem, *stages = refs
 
     loads = []
     k = 0
@@ -216,7 +216,7 @@
 
     big, small = lift_scale * lift_scale, 1.0 / (lift_scale * lift_scale)
 
-    def vertical(ref, c, start, length, before, after):
+    def vertical(ref, c, start, length, before, after, into):
         def window(b):
             body = ref[b, c, pl.ds(start, length), :]
             halo = jnp.where(
@@ -234,31 +234,21 @@
             else:
                 rough = rough * small
             smooth, rough = lifted(smooth, rough, shift_down, shift_up)
-            joined[half, c, pl.ds(0, length, stride=2), :] = smooth[:length]
-            joined[half, c, pl.ds(1, length, stride=2), :] = rough[:length]
-
-    def horizontal(tiles, load, store, last):
-        smooth = [load(0, c) for c in range(tiles + 1)]
-        rough = [load(1, c) for c in range(tiles + 1)]
-
-        def before(x):
-            turned = [pltpu.roll(t, 1, 1) for t in x]
-            return [jnp.where(lane == 0, turned[c - 1], turned[c]) for c in range(tiles + 1)]
-
-        def after(x):
-            turned = [pltpu.roll(t, LANES - 1, 1) for t in x]
-            return [
-                jnp.where(lane == LANES - 1, turned[(c + 1) % (tiles + 1)], turned[c])
-                for c in range(tiles + 1)
-            ]
-
-        def step(x, factor, y, z):
-            return [a - factor * (b + c) for a, b, c in zip(x, y, z)]
-
-        smooth = step(smooth, lift_delta, rough, before(rough))
-        rough = step(rough, lift_gamma, smooth, after(smooth))
-        smooth = step(smooth, lift_beta, rough, before(rough))
-        rough = step(rough, lift_alpha, smooth, after(smooth))
+            joined[half, c, pl.ds(into, length, stride=2), :] = smooth[:length]
+            joined[half, c, pl.ds(into + 1, length, stride=2), :] = rough[:length]
+
+    def rolled_before(x, n):
+        turned = [pltpu.roll(t, 1, 1) for t in x]
+        return [jnp.where(lane == 0, turned[c - 1], turned[c]) for c in range(n)]
+
+    def rolled_after(x, n):
+        turned = [pltpu.roll(t, LANES - 1, 1) for t in x]
+        return [jnp.where(lane == LANES - 1, turned[(c + 1) % n], turned[c]) for c in range(n)]
+
+    def step(x, factor, y, z):
+        return [a - factor * (b + c) for a, b, c in zip(x, y, z)]
+
+    def interleave(smooth, rough, tiles, store, last):
         for c in range(tiles if last else tiles + 1):
             first = jnp.where(low, smooth[c], rough[c])
             second = jnp.where(low, rough[c], smooth[c])
@@ -272,7 +262,61 @@
             else:
                 store(2 * c, jnp.where(low, left, right))
 
-    stores = []
+    def horizontal(tiles, load, store, last):
+        n = tiles + 1
+        smooth = [load(0, c) for c in range(n)]
+        rough = [load(1, c) for c in range(n)]
+        smooth = step(smooth, lift_delta, rough, rolled_before(rough, n))
+        rough = step(rough, lift_gamma, smooth, rolled_after(smooth, n))
+        smooth = step(smooth, lift_beta, rough, rolled_before(rough, n))
+        rough = step(rough, lift_alpha, smooth, rolled_after(smooth, n))
+        interleave(smooth, rough, tiles, store, last)
+
+    def pipelined(tiles, total, unroll, target, last, after_step):
+        n = tiles + 1
+        s1, r1, s2, r2 = stages
+        groups = total // (SUB * unroll)
+
+        def body(t, carry):
+            def rows_at(group, u):
+                first = jnp.clip(group, 0, groups - 1) * (SUB * unroll) + u * SUB
+                return pl.ds(pl.multiple_of(first, SUB), SUB)
+
+            def get(buffer, group, u):
+                slot = lax.rem(group + 8, 2)
+                return [buffer[slot, u, c] for c in range(n)]
+
+            def put(buffer, group, u, value):
+                slot = lax.rem(group + 8, 2)
+                for c in range(n):
+                    buffer[slot, u, c] = value[c]
+
+            for u in range(unroll):
+                into = rows_at(t - 4, u)
+
+                def store(c, value, into=into):
+                    target[c, into, :] = value
+
+                interleave(get(s2, t - 4, u), get(r2, t - 4, u), tiles, store, last)
+            for u in range(unroll):
+                smooth = get(s2, t - 3, u)
+                put(r2, t - 3, u, step(get(r1, t - 3, u), lift_alpha, smooth, rolled_after(smooth, n)))
+            for u in range(unroll):
+                rough = get(r1, t - 2, u)
+                put(s2, t - 2, u, step(get(s1, t - 2, u), lift_beta, rough, rolled_before(rough, n)))
+            for u in range(unroll):
+                smooth = get(s1, t - 1, u)
+                rough = [joined[1, c, rows_at(t - 1, u), :] for c in range(n)]
+                put(r1, t - 1, u, step(rough, lift_gamma, smooth, rolled_after(smooth, n)))
+            for u in range(unroll):
+                smooth = [joined[0, c, rows_at(t, u), :] for c in range(n)]
+                rough = [joined[1, c, rows_at(t, u), :] for c in range(n)]
+                put(s1, t, u, step(smooth, lift_delta, rough, rolled_before(rough, n)))
+            after_step(t - 4, groups)
+            return carry
+
+        lax.fori_loop(0, groups + 4, body, 0)
+
     for level, (height, width) in enumerate(sizes):
         tiles = width // LANES
         last = level == count - 1
@@ -288,21 +332,48 @@
             start = pl.multiple_of(i * rows, SUB)
             before = pl.multiple_of(jnp.where(i == 0, height, start - SUB), SUB)
             after = pl.multiple_of(start + rows, SUB)
+            into = pl.multiple_of(2 * start, SUB)
 
             def one_column(c, carry):
-                vertical(ref, c, start, rows, before, after)
+                vertical(ref, c, start, rows, before, after, into)
                 return carry
 
             lax.fori_loop(0, tiles + 1, one_column, 0)
+            return carry
+
+        lax.fori_loop(0, chunks, one_chunk, 0)
+
+        def store_copy(piece, c):
+            span = pl.ds(pl.multiple_of(piece * piece_rows, SUB), piece_rows)
+            return pltpu.make_async_copy(
+                finished.at[c, span, :],
+                out.at[span, pl.ds(c * LANES, LANES)],
+                store_sem.at[piece, c],
+            )
+
+        if tiles >= 4:
+            unroll = UNROLL if last else 2 * UNROLL
+
+            def after_step(group, groups):
+                if not last:
+                    return
+                every = piece_rows // (SUB * unroll)
+
+                @pl.when((group >= 0) & (lax.rem(group + every, every) == every - 1))
+                def _():
+                    for c in range(2 * tiles):
+                        store_copy(group // every, c).start()
+
+            pipelined(tiles, 2 * height, unroll, target, last, after_step)
+        else:
+            unroll = math.gcd(16, 2 * height // SUB)
 
             def one_row(t, carry):
                 for u in range(unroll):
-                    first = (t * unroll + u) * SUB
-                    where = pl.ds(pl.multiple_of(first, SUB), SUB)
-                    into = pl.ds(pl.multiple_of(2 * start + first, SUB), SUB)
-
-                    def store(c, value, into=into):
-                        target[c, into, :] = value
+                    where = pl.ds(pl.multiple_of((t * unroll + u) * SUB, SUB), SUB)
+
+                    def store(c, value, where=where):
+                        target[c, where, :] = value
 
                     def load(half, c, where=where):
                         return joined[half, c, where, :]
@@ -310,26 +381,12 @@
                     horizontal(tiles, load, store, last)
                 return carry
 
-            lax.fori_loop(0, 2 * rows // (SUB * unroll), one_row, 0)
-            return carry
-
-        if last:
-            for i in range(chunks):
-                one_chunk(i, 0)
-                span = pl.ds(2 * i * rows, 2 * rows)
-                for c in range(2 * tiles):
-                    copy = pltpu.make_async_copy(
-                        finished.at[c, span, :],
-                        out.at[span, pl.ds(c * LANES, LANES)],
-                        store_sem.at[len(stores)],
-                    )
-                    copy.start()
-                    stores.append(copy)
-        else:
-            lax.fori_loop(0, chunks, one_chunk, 0)
+            lax.fori_loop(0, 2 * height // (SUB * unroll), one_row, 0)
+
+        if not last:
 
             def edge_column(c, carry):
-                vertical(ref, c, height, SUB, height - SUB, 0)
+                vertical(ref, c, height, SUB, height - SUB, 0, 0)
                 return carry
 
             lax.fori_loop(0, tiles + 1, edge_column, 0)
@@ -343,8 +400,10 @@
                 target[c, pl.ds(2 * height, SUB), :] = value
 
             horizontal(tiles, load, store, False)
-    for copy in stores:
-        copy.wait()
+        else:
+            for piece in range(2 * height // piece_rows):
+                for c in range(2 * tiles):
+                    store_copy(piece, c).wait()
 
 
 def per_device(mesh_shape, coarse, *details):
@@ -383,9 +442,9 @@
     chunk_rows = 64
     height, width = sizes[-1]
     n_loads = sum(w // LANES for h, w in sizes) + sizes[0][1] // LANES
-    n_stores = (height // min(chunk_rows, height)) * (2 * width // LANES)
+    piece_rows = math.gcd(128, 2 * height)
     return pl.pallas_call(
-        functools.partial(synthesis, sizes, chunk_rows),
+        functools.partial(synthesis, sizes, chunk_rows, piece_rows),
         out_shape=shape(2 * height, 2 * width),
         in_specs=[anywhere] * n + [in_vmem] * len(halo_shapes),
         out_specs=anywhere,
@@ -393,11 +452,12 @@
             pltpu.VMEM((4, w // LANES + 1, h + SUB, LANES), f32) for h, w in sizes
         ]
         + [
-            pltpu.VMEM((2, width // LANES + 1, 2 * min(chunk_rows, height), LANES), f32),
+            pltpu.VMEM((2, width // LANES + 1, 2 * height, LANES), f32),
             pltpu.VMEM((2 * width // LANES, 2 * height, LANES), f32),
             pltpu.SemaphoreType.DMA((n_loads,)),
-            pltpu.SemaphoreType.DMA((n_stores,)),
-        ],
+            pltpu.SemaphoreType.DMA((2 * height // piece_rows, 2 * width // LANES)),
+        ]
+        + [pltpu.VMEM((2, 2 * UNROLL, width // LANES + 1, SUB, LANES), f32)] * 4,
         compiler_params=pltpu.CompilerParams(vmem_limit_bytes=56 * 1024 * 1024),
         name="synthesis",
     )(*arrays, *halos)

time: 51.7 us -> 42.4 us (0.82)
  Pallas kernels: 51.5 us -> 42.2 us
    pallas_call x1, Pallas kernels: 37.1 us -> 27.8 us  [per_device(): pl.pallas_call(functools.partial(synthesis, sizes, chunk_rows, piece_rows...]
where the time goes in v2:
time: 42.4 us; the launch traced here: 42.2 us
  Pallas kernels  42.2 us (100%)
    pallas_call x1, Pallas kernels, per_device(): pl.pallas_call(functools.partial(synthesis, sizes, chunk_rows, piece_rows...  27.8 us
    pallas_call x1, Pallas kernels, per_device(): pl.pallas_call(functools.partial(exchange, mesh_shape, levels), out_shape...  14.4 us

profile of v2, /device:TPU:0, one launch (start us, length us, event | category | flops | bytes accessed | tf_op | source)
XLA Modules:
  0.0 42.2 jit_solution(2785731367741407209)
XLA Ops:
  0.0 14.4 %exchange.1 = (f32[1,8,128]{2,1,0:T(8,128)}, f32[3,8,128]{2,1,0:T(8,128)}, f32[3,8,256]{2,1,0:T(8,128)}, f32[3,8,512]{2,1,0:T(8,128)}, f32[3,8,1024]{2,1,0:T(8,1...) custom-call(f32[1,64,128]{2,1,0:T(8,128)} %bitcast.1, ...), custom_call_target="tpu_custom_call" | custom-call | tf_op jit(solution)/shard_map/exchange/pallas_call | solution.py:422
  14.4 27.8 %synthesis.1 = f32[1024,2048]{1,0:T(8,128)} custom-call(f32[1,64,128]{2,1,0:T(8,128)} %bitcast.2, f32[3,64,128]{2,1,0:T(8,128)} %refs_1_.3, f32[3,128,256]{2,1,0:T(8,128)} %refs_2_.3, f32[3,256,512]{2,1,0:T(8,128)} %refs_3_.3, f32[3,512,1024]{2,1,0:T(8,128)} %refs_4_.3, f32[1,8,128]{2,1,0:T(8,128)} %get-tuple-element.21.refs_5_, ...), custom_call_target="tpu_custom_call" | custom-call | tf_op jit(solution)/shard_map/synthesis/pallas_call | solution.py:446
